TPU v7x, 32 devices: a whole 2x2x4 slice. The times are simulated.
32 devices in a mesh: dp: 8 (over z, x), tensor: 4 (over y, core).
Axes of the slice: x: 2, y: 2, z: 4, core: 2. Of those that a mesh axis runs over, the one named last changes fastest.
Arguments:
- logits: bfloat16 [16, 128, 19456], P('dp', None, 'tensor'), may hold values from -110 to 290
- token_ids: int32 [16, 128], P('dp'), may hold values from 0 to 19455
- response_mask: int32 [16, 128], P('dp'), may hold values 0 or 1
- lengths: int32 [16], P('dp'), may hold values from 16 to 128
- prompt_of: int32 [16], P('dp'), may hold values from 0 to 1, as said below
- old_logprob: float32 [16, 128], P('dp'), may hold values from -14 to -10
- ref_logprob: bfloat16 [16, 128], P(None, 'dp'), may hold values from -14 to -10
- advantages: float32 [16, 128], P('dp'), may hold values from -8 to 8
- returns: float32 [16, 128], P('dp'), may hold values from -6 to 6
- critic_hidden: bfloat16 [16, 128, 5120], P(None, 'dp', 'tensor'), may hold values from -6 to 6
- value_weight: bfloat16 [5120], P('tensor'), may hold values from -0.078125 to 0.078125
Outputs:
- token_loss: float32 [16, 128], P('dp')
- critic_grad: bfloat16 [16, 128, 5120], P(None, 'dp', 'tensor')
Inputs may be any that keep to these rules, and one draw needn't show every extreme that they name: `prompt_of`: each of the 2 prompts is named by exactly 8 sequences.
All inputs are finite; a program needn't handle non-finite values. No bound on the sum of `response_mask` on one device may be relied on, other than what follows from the above.
Results may differ from a plain program's by a relative error of at most 0.001.
Values may be sent and summed in bfloat16 or wider, within the bound.
No kernel may reach another device: no remote copies, remote signals or barrier semaphores. Data moves between devices by JAX's collectives and lax.ppermute only.
A program may use at most 64 MiB of HBM per device.

v0:
```python
import jax
import jax.numpy as jnp
from jax import lax
from jax.sharding import PartitionSpec as P

RESPONSES = 8


def per_device(
    logits,
    token_ids,
    response_mask,
    lengths,
    prompt_of,
    old_logprob,
    ref_logprob,
    advantages,
    returns,
    critic_hidden,
    value_weight,
):
    highest = lax.Precision.HIGHEST
    seq_rows, seq_len, vocab_width = logits.shape
    all_seqs, tile_len, feat_count = critic_hidden.shape
    dp_size = lax.axis_size("dp")
    head_weight = value_weight.astype(jnp.float32)
    tile_rows = critic_hidden.reshape(all_seqs * tile_len, feat_count)
    local_part = jnp.dot(tile_rows, value_weight, preferred_element_type=jnp.float32).reshape(
        all_seqs, tile_len
    )
    partial_value, ref_rows = (
        lax.all_to_all(local_part, "dp", split_axis=0, concat_axis=1, tiled=True),
        lax.all_to_all(
            ref_logprob.astype(jnp.float32), "dp", split_axis=0, concat_axis=1, tiled=True
        ),
    )
    position = lax.broadcasted_iota(jnp.int32, (seq_rows, seq_len), 1)
    live_mask = (response_mask * (position < lengths[:, None]).astype(jnp.int32)).astype(
        jnp.float32
    )
    prompt_count = seq_rows * dp_size // RESPONSES
    prompt_hot = (
        prompt_of[:, None] == lax.broadcasted_iota(jnp.int32, (seq_rows, prompt_count), 1)
    ).astype(jnp.float32)
    seq_tokens = jnp.sum(live_mask, axis=1)
    seq_total = jnp.sum(live_mask * advantages, axis=1)
    seq_square = jnp.sum(live_mask * advantages * advantages, axis=1)
    moments = jnp.dot(jnp.stack([seq_tokens, seq_total, seq_square]), prompt_hot, precision=highest)
    count_all, total_all, square_all = lax.psum((moments[0], moments[1], moments[2]), "dp")
    count_floor = jnp.maximum(count_all, 1.0)
    prompt_mean = total_all / count_floor
    prompt_var = (square_all - prompt_mean * total_all) / count_floor
    row_mean = jnp.dot(prompt_hot, prompt_mean, precision=highest)
    row_scale = lax.rsqrt(jnp.dot(prompt_hot, prompt_var, precision=highest) + 1.0)
    whitened = (advantages - row_mean[:, None]) * row_scale[:, None]
    local_top = jnp.max(logits, axis=2).astype(jnp.float32)
    local_sum = jnp.sum(jnp.exp(logits.astype(jnp.float32) - local_top[:, :, None]), axis=2)
    vocab_start = lax.axis_index("tensor") * vocab_width
    shifted = token_ids - vocab_start
    in_shard = (shifted >= 0) & (shifted < vocab_width)
    clipped_ids = jnp.clip(shifted, 0, vocab_width - 1)
    picked = jnp.take_along_axis(logits, clipped_ids[:, :, None], axis=2)[:, :, 0].astype(
        jnp.float32
    )
    target_part = jnp.where(in_shard, picked, 0.0)
    row_max = lax.pmax(local_top, "tensor")
    rescaled = local_sum * jnp.exp(local_top - row_max)
    total_sum, target_logit, value_pred = lax.psum((rescaled, target_part, partial_value), "tensor")
    logprob = target_logit - (row_max + jnp.log(total_sum))
    prob_ratio = jnp.exp(jnp.clip(logprob - old_logprob, -20.0, 20.0))
    surrogate = jnp.maximum(-whitened * prob_ratio, -whitened * jnp.clip(prob_ratio, 0.8, 1.2))
    surrogate = jnp.where(whitened < 0.0, jnp.minimum(surrogate, -3.0 * whitened), surrogate)
    ref_drift = jnp.clip(ref_rows - logprob, -20.0, 20.0)
    penalty = jnp.clip(jnp.exp(ref_drift) - ref_drift - 1.0, -10.0, 10.0)
    value_error = value_pred - returns
    token_loss = live_mask * (surrogate + 0.1 * penalty + 0.25 * value_error * value_error)
    grad_coeff = 32.0 * live_mask * value_error
    returned = lax.all_to_all(grad_coeff, "dp", split_axis=1, concat_axis=0, tiled=True)
    critic_grad = (returned[:, :, None] * head_weight[None, None, :]).astype(jnp.bfloat16)
    return (token_loss, critic_grad)


def solution(mesh):
    in_specs = (
        P("dp", None, "tensor"),
        P("dp", None),
        P("dp", None),
        P("dp"),
        P("dp"),
        P("dp", None),
        P(None, "dp"),
        P("dp", None),
        P("dp", None),
        P(None, "dp", "tensor"),
        P("tensor"),
    )
    out_specs = (P("dp", None), P(None, "dp", "tensor"))
    return jax.shard_map(
        per_device, mesh=mesh, in_specs=in_specs, out_specs=out_specs, check_vma=False
    )
```

profile of v0, /device:TPU:0, one launch (start us, length us, event | category | flops | bytes accessed | tf_op | source)
XLA Modules:
  0.0 71.6 jit_solution(9083070051270361440)
XLA Ops:
  0.7 1.4 %convert.1 = f32[8,2,16]{2,1,0:T(2,128)} convert(bf16[8,2,16]{2,1,0:T(2,128)(2,1)} %bitcast.45) | non-fusion elementwise | flops 256 | bytes 1536 | tf_op jit(solution)/shard_map/all_to_all | solution.py:33
  2.1 7.3 %all-to-all-start = ((f32[8,2,16]{2,1,0:T(2,128)}), f32[8,2,16]{2,1,0:T(2,128)S(1)}, u32[]{:S(2)}, u32[]{:S(2)}) async-start(f32[8,2,16]{2,1,0:T(2,128)} %convert.1), calls=%async_computation | async-start | bytes 16384 | tf_op jit(solution)/shard_map/all_to_all | solution.py:33
  9.4 2.1 %reduce_max.9 = bf16[2,128]{1,0:T(2,128)(2,1)S(1)} reduce(bf16[2,128,4864]{2,1,0:T(8,128)(2,1)} %param.11, bf16[]{:T(256)} %constant.27.clone.1), dimensions={2}, to_apply=%region_7.0 | reduce | flops 1244928 | bytes 2490882 | tf_op jit(solution)/shard_map/reduce_max | solution.py:56
  11.6 6.6 %pmax.7 = f32[2,128]{1,0:T(2,128)S(1)} all-reduce(bf16[2,128]{1,0:T(2,128)(2,1)S(1)} %reduce_max.9), channel_id=1, replica_groups=mesh['dp'=8,'tensor'=4] {'tensor'}, use_global_device_ids=true, to_apply=%region_8.9 | all-reduce | flops 256 | bytes 1536 | tf_op jit(solution)/shard_map/pmax | solution.py:66
  18.2 1.0 %exponential_reduce_fusion = f32[2,128]{1,0:T(2,128)S(1)} fusion(bf16[2,128,4864]{2,1,0:T(8,128)(2,1)S(1)} %copy-done.1, f32[2,128]{1,0:T(2,128)S(1)} %convert_element_type.27), kind=kLoop, calls=%fused_computation.1 | loop fusion | flops 3735296 | bytes 2492416 | tf_op jit(solution)/shard_map/reduce_sum | solution.py:57
  19.3 1.5 %fusion.2 = f32[1,8,2,16]{3,0,2,1:T(1,128)} fusion(bf16[8,2,16,1280]{3,2,1,0:T(8,128)(2,1)S(1)} %bitcast.41, bf16[1280,1,1,1]{0,1,2,3:T(2,128)(2,1)S(1)} %reshape.68), kind=kOutput, calls=%fused_computation.7 | convolution fusion | flops 655360 | bytes 658944 | tf_op jit(solution)/shard_map/dot_general | solution.py:28
  20.8 2.8 %gather_fusion = bf16[256]{0:T(256)(128)(2,1)S(1)} fusion(bf16[2,128,4864]{2,1,0:T(8,128)(2,1)S(1)} %copy-done.1, s32[256]{0:T(256)S(1)} %fusion.18), kind=kCustom, calls=%fused_computation | custom fusion | bytes 4096 | tf_op jit(solution)/shard_map/jit(take_along_axis)/gather | solution.py:62
  23.6 5.4 %all-to-all-start.1 = ((f32[8,2,16]{2,1,0:T(2,128)}), f32[8,2,16]{2,1,0:T(2,128)S(1)}, u32[]{:S(2)}, u32[]{:S(2)}) async-start(f32[8,2,16]{2,1,0:T(2,128)} %bitcast.16), calls=%async_computation.1 | async-start | bytes 16384 | tf_op jit(solution)/shard_map/all_to_all | solution.py:32
  29.1 0.1 all_to_all.44
  29.1 6.4 %all-to-all-done.1 = f32[8,2,16]{2,1,0:T(2,128)S(1)} async-done(((f32[8,2,16]{2,1,0:T(2,128)}), f32[8,2,16]{2,1,0:T(2,128)S(1)}, u32[]{:S(2)}, u32[]{:S(2)}) %all-to-all-start.1) | async-done | bytes 1056 | tf_op jit(solution)/shard_map/all_to_all | solution.py:32
  35.5 0.1 all_to_all.47
  35.6 5.6 %all-reduce.1 = (f32[2,128]{1,0:T(2,128)S(1)}, f32[2,128]{1,0:T(2,128)S(1)}, f32[2,128]{1,0:T(2,128)S(1)}) all-reduce(f32[2,128]{1,0:T(2,128)S(1)} %and_select_fusion.1, f32[2,128]{1,0:T(2,128)S(1)} %exponential_multiply_fusion, f32[2,128]{1,0:T(2,128)S(1)} %all_to_all.47), channel_id=1, replica_groups=mesh['dp'=8,'tensor'=4] {'tensor'}, use_global_device_ids=true, to_apply=%region_6.0 | all-reduce | flops 768 | bytes 6144 | tf_op jit(solution)/shard_map/psum | solution.py:68
  41.4 0.1 multiply_reduce_fusion.1
  41.5 0.3 fusion.4
  41.8 0.2 slice_reduce_fusion.1
  42.0 17.7 %all-reduce = (f32[2]{0:T(128)S(1)}, f32[2]{0:T(128)S(1)}, f32[2]{0:T(128)S(1)}) all-reduce(f32[2]{0:T(128)S(1)} %get-tuple-element.5, f32[2]{0:T(128)S(1)} %get-tuple-element.6, f32[2]{0:T(128)S(1)} %get-tuple-element.4), channel_id=1, replica_groups=mesh['dp'=8,'tensor'=4] {'dp'}, use_global_device_ids=true, to_apply=%region_5.0 | all-reduce | flops 6 | bytes 48 | tf_op jit(solution)/shard_map/psum | solution.py:49
  59.7 0.2 convolution_bitcast_fusion.1
  59.9 0.2 fusion.1
  60.1 0.1 all_to_all.48
  60.2 0.6 copy.19
  60.8 3.3 %all-to-all-start.2 = ((f32[2,8,16]{2,0,1:T(2,128)}), f32[2,8,16]{2,0,1:T(2,128)S(1)}, u32[]{:S(2)}, u32[]{:S(2)}) async-start(f32[2,8,16]{2,0,1:T(2,128)} %copy.19), calls=%async_computation.2 | async-start | bytes 16384 | tf_op jit(solution)/shard_map/all_to_all | solution.py:78
  64.1 0.6 fusion.22
  64.8 5.8 %all-to-all-done.2 = f32[2,8,16]{2,0,1:T(2,128)S(1)} async-done(((f32[2,8,16]{2,0,1:T(2,128)}), f32[2,8,16]{2,0,1:T(2,128)S(1)}, u32[]{:S(2)}, u32[]{:S(2)}) %all-to-all-start.2) | async-done | bytes 1056 | tf_op jit(solution)/shard_map/all_to_all | solution.py:78
  70.6 1.0 %multiply_convert_fusion = bf16[16,16,1280]{2,1,0:T(8,128)(2,1)} fusion(f32[1280]{0:T(1024)S(1)} %convert_element_type.29, f32[16,16]{1,0:T(8,128)S(1)} %bitcast.42), kind=kLoop, calls=%fused_computation.2 | loop fusion | flops 655360 | bytes 661504 | tf_op jit(solution)/shard_map/convert_element_type | solution.py:79
  (35 shorter events, 0.2 us)
Async XLA Ops:
  0.6 18.6 %copy-start = (bf16[16,16,1280]{2,1,0:T(8,128)(2,1)S(1)}, bf16[16,16,1280]{2,1,0:T(8,128)(2,1)}, u32[]{:S(2)}) copy-start(bf16[16,16,1280]{2,1,0:T(8,128)(2,1)} %param.20) | copy-start | bytes 1966084
  0.6 17.6 %copy-start.1 = (bf16[2,128,4864]{2,1,0:T(8,128)(2,1)S(1)}, bf16[2,128,4864]{2,1,0:T(8,128)(2,1)}, u32[]{:S(2)}) copy-start(bf16[2,128,4864]{2,1,0:T(8,128)(2,1)} %param.11) | copy-start | bytes 7471108
  2.1 21.5 %all-to-all-start = ((f32[8,2,16]{2,1,0:T(2,128)}), f32[8,2,16]{2,1,0:T(2,128)S(1)}, u32[]{:S(2)}, u32[]{:S(2)}) async-start(f32[8,2,16]{2,1,0:T(2,128)} %convert.1), calls=%async_computation | async-start | bytes 16384 | tf_op jit(solution)/shard_map/all_to_all | solution.py:33
  9.4 9.8 %copy-start.2 = (bf16[1280]{0:T(1024)(128)(2,1)S(1)}, bf16[1280]{0:T(1024)(128)(2,1)}, u32[]{:S(2)}) copy-start(bf16[1280]{0:T(1024)(128)(2,1)} %param.21) | copy-start | bytes 7684
  9.4 9.8 %copy-start.3 = (s32[2,128]{1,0:T(2,128)S(1)}, s32[2,128]{1,0:T(2,128)}, u32[]{:S(2)}) copy-start(s32[2,128]{1,0:T(2,128)} %param.12) | copy-start | bytes 3076
  11.5 29.7 %copy-start.5 = (f32[2,128]{1,0:T(2,128)S(1)}, f32[2,128]{1,0:T(2,128)}, u32[]{:S(2)}) copy-start(f32[2,128]{1,0:T(2,128)} %param.19) | copy-start | bytes 3076
  11.5 29.7 %copy-start.6 = (s32[2,128]{1,0:T(2,128)S(1)}, s32[2,128]{1,0:T(2,128)}, u32[]{:S(2)}) copy-start(s32[2,128]{1,0:T(2,128)} %param.13) | copy-start | bytes 3076
  11.5 29.7 %copy-start.8 = (s32[2]{0:T(128)S(1)}, s32[2]{0:T(128)}, u32[]{:S(2)}) copy-start(s32[2]{0:T(128)} %param.14) | copy-start | bytes 28
  11.6 29.8 %copy-start.4 = (f32[2,128]{1,0:T(2,128)S(1)}, f32[2,128]{1,0:T(2,128)}, u32[]{:S(2)}) copy-start(f32[2,128]{1,0:T(2,128)} %param.18) | copy-start | bytes 3076
  11.6 29.9 %copy-start.9 = (s32[2]{0:T(128)S(1)}, s32[2]{0:T(128)}, u32[]{:S(2)}) copy-start(s32[2]{0:T(128)} %param.15) | copy-start | bytes 28
  11.6 52.5 %copy-start.7 = (f32[2,128]{1,0:T(2,128)S(1)}, f32[2,128]{1,0:T(2,128)}, u32[]{:S(2)}) copy-start(f32[2,128]{1,0:T(2,128)} %param.16) | copy-start | bytes 3076
  23.6 12.0 %all-to-all-start.1 = ((f32[8,2,16]{2,1,0:T(2,128)}), f32[8,2,16]{2,1,0:T(2,128)S(1)}, u32[]{:S(2)}, u32[]{:S(2)}) async-start(f32[8,2,16]{2,1,0:T(2,128)} %bitcast.16), calls=%async_computation.1 | async-start | bytes 16384 | tf_op jit(solution)/shard_map/all_to_all | solution.py:32
  60.8 9.8 %all-to-all-start.2 = ((f32[2,8,16]{2,0,1:T(2,128)}), f32[2,8,16]{2,0,1:T(2,128)S(1)}, u32[]{:S(2)}, u32[]{:S(2)}) async-start(f32[2,8,16]{2,0,1:T(2,128)} %copy.19), calls=%async_computation.2 | async-start | bytes 16384 | tf_op jit(solution)/shard_map/all_to_all | solution.py:78
where the time goes:
time: 71.9 us; the launch traced here: 71.6 us
  blocking collectives  30 us (42%)
  starting transfers between devices  16 us (22%)
  waiting for transfers between devices  12.2 us (17%)
  other arithmetic  6.42 us (9%)
  local copies, waits for them, and re-layouts  3.95 us (5%)
  matrix products  2.1 us (3%)
  between operations  0.83 us (1%)
    psum x1, blocking collectives, per_device(): lax.psum((moments[0], moments[1], moments[2]), 'dp')  17.7 us
    all_to_all x1, starting transfers between devices, per_device(): lax.all_to_all(ref_logprob.astype(jnp.float32), 'dp', split_axis=0, conca...  7.28 us
    pmax x1, blocking collectives, per_device(): row_max = lax.pmax(local_top, 'tensor')  6.63 us
    all_to_all x1, waiting for transfers between devices, per_device(): lax.all_to_all(local_part, 'dp', split_axis=0, concat_axis=1, tiled=True)  6.41 us
    all_to_all x1, waiting for transfers between devices, per_device(): lax.all_to_all(grad_coeff, 'dp', split_axis=1, concat_axis=0, tiled=True)  5.8 us
    psum x1, blocking collectives, per_device(): lax.psum((rescaled, target_part, partial_value), 'tensor')  5.64 us
    all_to_all x1, starting transfers between devices, per_device(): lax.all_to_all(local_part, 'dp', split_axis=0, concat_axis=1, tiled=True)  5.43 us
    all_to_all x1, starting transfers between devices, per_device(): lax.all_to_all(grad_coeff, 'dp', split_axis=1, concat_axis=0, tiled=True)  3.33 us
  transfers between devices with their start and end apart: 3, of which 2 were waited for; matrix products, arithmetic and copies ran while one was open for 11% of the time, Pallas kernels for 0%

commit v1 on v0

--- a/solution.py
+++ b/solution.py
@@ -4,6 +4,13 @@
 from jax.sharding import PartitionSpec as P
 
 RESPONSES = 8
+
+
+def cut_face(own_rows):
+    outcome_arr = jax.lax.all_to_all(
+        jnp.stack(jnp.split(own_rows, jax.lax.axis_size("dp"), axis=0), 0), "dp", 0, 0
+    )
+    return jnp.concatenate(outcome_arr, 1)
 
 
 def per_device(
@@ -29,7 +36,7 @@
         all_seqs, tile_len
     )
     partial_value, ref_rows = (
-        lax.all_to_all(local_part, "dp", split_axis=0, concat_axis=1, tiled=True),
+        cut_face(local_part),
         lax.all_to_all(
             ref_logprob.astype(jnp.float32), "dp", split_axis=0, concat_axis=1, tiled=True
         ),

time: 71.9 us -> 76 us (1.057)
  local copies, waits for them, and re-layouts: 3.95 us -> 9.25 us
  matrix products: 2.1 us -> 0.87 us
    unnamed x23 -> x30, local copies, waits for them, and re-layouts: 0.07 us -> 4.09 us
    dot_general x1, matrix products: 1.47 us -> 0.24 us  [per_device(): jnp.dot(tile_rows, value_weight, preferred_element_type=jnp.float32)]
  transfers between devices with their start and end apart: 3 -> 3, of which waited for: 2 -> 2; matrix products, arithmetic and copies ran while one was open for 11% -> 16% of each run, Pallas kernels for 0% -> 0%
where the time goes in v1:
time: 76 us; the launch traced here: 75.7 us
  blocking collectives  30 us (39%)
  starting transfers between devices  16 us (21%)
  waiting for transfers between devices  12.2 us (16%)
  local copies, waits for them, and re-layouts  9.25 us (12%)
  other arithmetic  6.41 us (8%)
  matrix products  0.87 us (1%)
  between operations  0.87 us (1%)
    psum x1, blocking collectives, per_device(): lax.psum((moments[0], moments[1], moments[2]), 'dp')  17.7 us
    all_to_all x1, starting transfers between devices, per_device(): lax.all_to_all(ref_logprob.astype(jnp.float32), 'dp', split_axis=0, conca...  7.28 us
    pmax x1, blocking collectives, per_device(): row_max = lax.pmax(local_top, 'tensor')  6.63 us
    all_to_all x1, waiting for transfers between devices, cut_face(): jax.lax.all_to_all(jnp.stack(jnp.split(own_rows, jax.lax.axis_size('dp'),...  6.41 us
    all_to_all x1, waiting for transfers between devices, per_device(): lax.all_to_all(grad_coeff, 'dp', split_axis=1, concat_axis=0, tiled=True)  5.8 us
    psum x1, blocking collectives, per_device(): lax.psum((rescaled, target_part, partial_value), 'tensor')  5.64 us
    all_to_all x1, starting transfers between devices, cut_face(): jax.lax.all_to_all(jnp.stack(jnp.split(own_rows, jax.lax.axis_size('dp'),...  5.43 us
    unnamed x30, local copies, waits for them, and re-layouts  4.09 us
  transfers between devices with their start and end apart: 3, of which 2 were waited for; matrix products, arithmetic and copies ran while one was open for 16% of the time, Pallas kernels for 0%

profile of v1, /device:TPU:0, one launch (start us, length us, event | category | flops | bytes accessed | tf_op | source)
XLA Modules:
  0.0 75.7 jit_solution(8027013318658561234)
XLA Ops:
  0.7 1.4 %convert.1 = f32[8,2,16]{2,1,0:T(2,128)} convert(bf16[8,2,16]{2,1,0:T(2,128)(2,1)} %bitcast.43) | non-fusion elementwise | flops 256 | bytes 1536 | tf_op jit(solution)/shard_map/all_to_all | solution.py:40
  2.1 7.3 %all-to-all-start = ((f32[8,2,16]{2,1,0:T(2,128)}), f32[8,2,16]{2,1,0:T(2,128)S(1)}, u32[]{:S(2)}, u32[]{:S(2)}) async-start(f32[8,2,16]{2,1,0:T(2,128)} %convert.1), calls=%async_computation | async-start | bytes 16384 | tf_op jit(solution)/shard_map/all_to_all | solution.py:40
  9.4 2.1 %reduce_max.9 = bf16[2,128]{1,0:T(2,128)(2,1)S(1)} reduce(bf16[2,128,4864]{2,1,0:T(8,128)(2,1)} %param.11, bf16[]{:T(256)} %constant.27.clone.1), dimensions={2}, to_apply=%region_7.0 | reduce | flops 1244928 | bytes 2490882 | tf_op jit(solution)/shard_map/reduce_max | solution.py:63
  11.6 6.6 %pmax.7 = f32[2,128]{1,0:T(2,128)S(1)} all-reduce(bf16[2,128]{1,0:T(2,128)(2,1)S(1)} %reduce_max.9), channel_id=1, replica_groups=mesh['dp'=8,'tensor'=4] {'tensor'}, use_global_device_ids=true, to_apply=%region_8.9 | all-reduce | flops 256 | bytes 1536 | tf_op jit(solution)/shard_map/pmax | solution.py:73
  18.2 1.0 %exponential_reduce_fusion = f32[2,128]{1,0:T(2,128)S(1)} fusion(bf16[2,128,4864]{2,1,0:T(8,128)(2,1)S(1)} %copy-done.1, f32[2,128]{1,0:T(2,128)S(1)} %convert_element_type.27), kind=kLoop, calls=%fused_computation.1 | loop fusion | flops 3735296 | bytes 2492416 | tf_op jit(solution)/shard_map/reduce_sum | solution.py:64
  20.3 0.6 constant_dynamic-update-slice_fusion.7
  20.9 0.6 constant_dynamic-update-slice_fusion.6
  21.5 0.6 constant_dynamic-update-slice_fusion.5
  22.1 0.6 constant_dynamic-update-slice_fusion.4
  22.6 0.6 constant_dynamic-update-slice_fusion.3
  23.2 0.6 constant_dynamic-update-slice_fusion.2
  23.7 0.6 constant_dynamic-update-slice_fusion.1
  24.3 0.6 constant_dynamic-update-slice_fusion
  24.9 2.8 %gather_fusion = bf16[256]{0:T(256)(128)(2,1)S(1)} fusion(bf16[2,128,4864]{2,1,0:T(8,128)(2,1)S(1)} %copy-done.1, s32[256]{0:T(256)S(1)} %fusion.16), kind=kCustom, calls=%fused_computation | custom fusion | bytes 4096 | tf_op jit(solution)/shard_map/jit(take_along_axis)/gather | solution.py:69
  27.7 5.4 %all-to-all-start.1 = ((f32[8,2,16]{2,1,0:T(2,128)}), f32[8,2,16]{2,1,0:T(2,128)S(1)}, u32[]{:S(2)}, u32[]{:S(2)}) async-start(f32[8,2,16]{2,1,0:T(2,128)} %constant_dynamic-update-slice_fusion), calls=%async_computation.1 | async-start | bytes 16384 | tf_op jit(solution)/shard_map/all_to_all | solution.py:10
  33.2 6.4 %all-to-all-done.1 = f32[8,2,16]{2,1,0:T(2,128)S(1)} async-done(((f32[8,2,16]{2,1,0:T(2,128)}), f32[8,2,16]{2,1,0:T(2,128)S(1)}, u32[]{:S(2)}, u32[]{:S(2)}) %all-to-all-start.1) | async-done | bytes 1056 | tf_op jit(solution)/shard_map/all_to_all | solution.py:10
  39.7 5.6 %all-reduce.1 = (f32[2,128]{1,0:T(2,128)S(1)}, f32[2,128]{1,0:T(2,128)S(1)}, f32[2,128]{1,0:T(2,128)S(1)}) all-reduce(f32[2,128]{1,0:T(2,128)S(1)} %and_select_fusion.1, f32[2,128]{1,0:T(2,128)S(1)} %exponential_multiply_fusion, f32[2,128]{1,0:T(2,128)S(1)} %reshape.136), channel_id=1, replica_groups=mesh['dp'=8,'tensor'=4] {'tensor'}, use_global_device_ids=true, to_apply=%region_6.0 | all-reduce | flops 768 | bytes 6144 | tf_op jit(solution)/shard_map/psum | solution.py:75
  45.6 0.3 fusion.2
  46.1 17.7 %all-reduce = (f32[2]{0:T(128)S(1)}, f32[2]{0:T(128)S(1)}, f32[2]{0:T(128)S(1)}) all-reduce(f32[2]{0:T(128)S(1)} %get-tuple-element.5, f32[2]{0:T(128)S(1)} %get-tuple-element.6, f32[2]{0:T(128)S(1)} %get-tuple-element.4), channel_id=1, replica_groups=mesh['dp'=8,'tensor'=4] {'dp'}, use_global_device_ids=true, to_apply=%region_5.0 | all-reduce | flops 6 | bytes 48 | tf_op jit(solution)/shard_map/psum | solution.py:56
  64.3 0.6 copy.22
  64.9 3.3 %all-to-all-start.2 = ((f32[2,8,16]{2,0,1:T(2,128)}), f32[2,8,16]{2,0,1:T(2,128)S(1)}, u32[]{:S(2)}, u32[]{:S(2)}) async-start(f32[2,8,16]{2,0,1:T(2,128)} %copy.22), calls=%async_computation.2 | async-start | bytes 16384 | tf_op jit(solution)/shard_map/all_to_all | solution.py:85
  68.2 0.6 fusion.20
  68.9 5.8 %all-to-all-done.2 = f32[2,8,16]{2,0,1:T(2,128)S(1)} async-done(((f32[2,8,16]{2,0,1:T(2,128)}), f32[2,8,16]{2,0,1:T(2,128)S(1)}, u32[]{:S(2)}, u32[]{:S(2)}) %all-to-all-start.2) | async-done | bytes 1056 | tf_op jit(solution)/shard_map/all_to_all | solution.py:85
  74.7 1.0 %multiply_convert_fusion = bf16[16,16,1280]{2,1,0:T(8,128)(2,1)} fusion(f32[1280]{0:T(1024)S(1)} %convert_element_type.29, f32[16,16]{1,0:T(8,128)S(1)} %bitcast.39), kind=kLoop, calls=%fused_computation.2 | loop fusion | flops 655360 | bytes 661504 | tf_op jit(solution)/shard_map/convert_element_type | solution.py:86
  (52 shorter events, 2.1 us)
Async XLA Ops:
  0.6 18.7 %copy-start = (bf16[16,16,1280]{2,1,0:T(8,128)(2,1)S(1)}, bf16[16,16,1280]{2,1,0:T(8,128)(2,1)}, u32[]{:S(2)}) copy-start(bf16[16,16,1280]{2,1,0:T(8,128)(2,1)} %param.20) | copy-start | bytes 1966084
  0.6 17.6 %copy-start.1 = (bf16[2,128,4864]{2,1,0:T(8,128)(2,1)S(1)}, bf16[2,128,4864]{2,1,0:T(8,128)(2,1)}, u32[]{:S(2)}) copy-start(bf16[2,128,4864]{2,1,0:T(8,128)(2,1)} %param.11) | copy-start | bytes 7471108
  2.1 25.6 %all-to-all-start = ((f32[8,2,16]{2,1,0:T(2,128)}), f32[8,2,16]{2,1,0:T(2,128)S(1)}, u32[]{:S(2)}, u32[]{:S(2)}) async-start(f32[8,2,16]{2,1,0:T(2,128)} %convert.1), calls=%async_computation | async-start | bytes 16384 | tf_op jit(solution)/shard_map/all_to_all | solution.py:40
  9.4 9.8 %copy-start.3 = (s32[2,128]{1,0:T(2,128)S(1)}, s32[2,128]{1,0:T(2,128)}, u32[]{:S(2)}) copy-start(s32[2,128]{1,0:T(2,128)} %param.12) | copy-start | bytes 3076
  9.4 9.9 %copy-start.2 = (bf16[1280]{0:T(1024)(128)(2,1)S(1)}, bf16[1280]{0:T(1024)(128)(2,1)}, u32[]{:S(2)}) copy-start(bf16[1280]{0:T(1024)(128)(2,1)} %param.21) | copy-start | bytes 7684
  11.5 33.9 %copy-start.5 = (f32[2,128]{1,0:T(2,128)S(1)}, f32[2,128]{1,0:T(2,128)}, u32[]{:S(2)}) copy-start(f32[2,128]{1,0:T(2,128)} %param.19) | copy-start | bytes 3076
  11.5 33.9 %copy-start.6 = (s32[2,128]{1,0:T(2,128)S(1)}, s32[2,128]{1,0:T(2,128)}, u32[]{:S(2)}) copy-start(s32[2,128]{1,0:T(2,128)} %param.13) | copy-start | bytes 3076
  11.5 33.8 %copy-start.8 = (s32[2]{0:T(128)S(1)}, s32[2]{0:T(128)}, u32[]{:S(2)}) copy-start(s32[2]{0:T(128)} %param.14) | copy-start | bytes 28
  11.6 33.9 %copy-start.4 = (f32[2,128]{1,0:T(2,128)S(1)}, f32[2,128]{1,0:T(2,128)}, u32[]{:S(2)}) copy-start(f32[2,128]{1,0:T(2,128)} %param.18) | copy-start | bytes 3076
  11.6 34.1 %copy-start.9 = (s32[2]{0:T(128)S(1)}, s32[2]{0:T(128)}, u32[]{:S(2)}) copy-start(s32[2]{0:T(128)} %param.15) | copy-start | bytes 28
  11.6 56.6 %copy-start.7 = (f32[2,128]{1,0:T(2,128)S(1)}, f32[2,128]{1,0:T(2,128)}, u32[]{:S(2)}) copy-start(f32[2,128]{1,0:T(2,128)} %param.16) | copy-start | bytes 3076
  27.7 12.0 %all-to-all-start.1 = ((f32[8,2,16]{2,1,0:T(2,128)}), f32[8,2,16]{2,1,0:T(2,128)S(1)}, u32[]{:S(2)}, u32[]{:S(2)}) async-start(f32[8,2,16]{2,1,0:T(2,128)} %constant_dynamic-update-slice_fusion), calls=%async_computation.1 | async-start | bytes 16384 | tf_op jit(solution)/shard_map/all_to_all | solution.py:10
  64.9 9.8 %all-to-all-start.2 = ((f32[2,8,16]{2,0,1:T(2,128)}), f32[2,8,16]{2,0,1:T(2,128)S(1)}, u32[]{:S(2)}, u32[]{:S(2)}) async-start(f32[2,8,16]{2,0,1:T(2,128)} %copy.22), calls=%async_computation.2 | async-start | bytes 16384 | tf_op jit(solution)/shard_map/all_to_all | solution.py:85
